TPU v7x, 256 devices: a 2x2x32 block of a 4x8x32 slice. The times are simulated.
256 devices in a mesh: group: 4 (over y, x), col: 64 (over z, core).
Axes of the slice: x: 2, y: 2, z: 32, core: 2. Of those that a mesh axis runs over, the one named last changes fastest.
The devices are a block of a 4x8x32 slice.
Arguments:
- homolog_embedding: bfloat16 [384, 256, 256], P('group', 'col'), parts along dimension 0, may hold values from -6 to 6
- left_factor_matrix: bfloat16 [256, 32], replicated, may hold values from -0.375 to 0.375
- right_factor_matrix: bfloat16 [256, 32], replicated, may hold values from -0.375 to 0.375
- decoder: bfloat16 [1024, 128], replicated, may hold values from -2 to 2
- pair_output_bias: float32 [128], replicated, may hold values from -3 to 3
- pair_output_gradient: bfloat16 [1024, 256, 128], P('group', 'col'), parts along dimension 0, may hold values from -16 to 16
Outputs:
- first_operand_gradient: float32 [384, 256, 32], P('group', 'col'), parts along dimension 0
- second_operand_gradient: float32 [384, 256, 32], P('group', 'col'), parts along dimension 0
- alignment_gradient: bfloat16 [384, 256, 256], P('group', 'col'), parts along dimension 0
There are 4 independent parts, one for each index of `group`. A program takes and returns all parts, laid end to end along the dimension named above; an argument that names none is the same for every part. Nothing has to cross between parts.
All inputs are finite; a program needn't handle non-finite values.
Results may differ from a plain program's by a relative error of at most 0.0083.
Values may be sent and summed in bfloat16 or wider, within the bound.
No kernel may reach another device: no remote copies, remote signals or barrier semaphores. Data moves between devices by JAX's collectives and lax.ppermute only.
A program may use at most 64 MiB of HBM per device.

v0:
```python
import jax
import jax.numpy as jnp
from jax import lax
from jax.sharding import PartitionSpec as P


def in_one_piece(arrays, axis, dim, along):
    widths = [a.shape[along] for a in arrays]
    both = jnp.concatenate(arrays, axis=along)
    whole = lax.all_gather(both, axis, axis=dim, tiled=True)
    return tuple(jnp.split(whole, [sum(widths[:k]) for k in range(1, len(widths))], axis=along))


def per_device(
    homolog_embedding,
    left_factor_matrix,
    right_factor_matrix,
    decoder,
    pair_output_bias,
    pair_output_gradient,
):
    alignment_row_count, local_residue_start, alignment_channel_width = homolog_embedding.shape
    operand_channel_width = left_factor_matrix.shape[1]
    channels = decoder.shape[1]
    residue_total_count = local_residue_start * lax.axis_size("col")
    reciprocal_rows = 1.0 / alignment_row_count
    block_res = local_residue_start * max(1, 96 // local_residue_start)
    alignment_flattened_rows = homolog_embedding.reshape(
        alignment_row_count * local_residue_start, alignment_channel_width
    )
    first_operand_rows = (
        jnp.dot(alignment_flattened_rows, left_factor_matrix, preferred_element_type=jnp.float32)
        .astype(jnp.bfloat16)
        .reshape(alignment_row_count, local_residue_start * operand_channel_width)
    )
    second_operand_rows = (
        jnp.dot(alignment_flattened_rows, right_factor_matrix, preferred_element_type=jnp.float32)
        .astype(jnp.bfloat16)
        .reshape(alignment_row_count, local_residue_start * operand_channel_width)
    )
    second_operand_local = second_operand_rows.reshape(
        alignment_row_count, local_residue_start, operand_channel_width
    )

    def outer_slopes(slope_rows, rows_by_length, col_span):
        backward = (
            jnp.dot(slope_rows, decoder.T, preferred_element_type=jnp.float32) * reciprocal_rows
        )
        return backward.astype(jnp.bfloat16).reshape(
            rows_by_length, col_span, operand_channel_width, operand_channel_width
        )

    offset_col = jnp.int32(0)
    second_operand_gradient = jnp.zeros(
        (alignment_row_count, local_residue_start, operand_channel_width), jnp.float32
    )
    stored = jnp.zeros((residue_total_count, local_residue_start * channels), jnp.bfloat16)
    left_segment, right_segment = in_one_piece(
        (first_operand_rows, second_operand_rows), "col", 1, 0
    )
    right_whole = right_segment
    piece_res = left_segment.shape[1] // operand_channel_width
    first_res = offset_col // operand_channel_width
    collected = []
    for split_offset in range(0, piece_res, block_res):
        split_rows_by_length = min(block_res, piece_res - split_offset)
        split_left_block = left_segment[
            :,
            split_offset
            * operand_channel_width : (split_offset + split_rows_by_length)
            * operand_channel_width,
        ].reshape(alignment_row_count, split_rows_by_length, operand_channel_width)
        collected.append((split_rows_by_length, split_left_block, first_res + split_offset))
    for rows_by_length, left_block, first_row in collected:
        products = (
            jnp.einsum(
                "sic,sjd->ijcd",
                left_block,
                second_operand_local,
                preferred_element_type=jnp.float32,
            )
            * reciprocal_rows
        )
        products = products.astype(jnp.bfloat16).reshape(
            rows_by_length * local_residue_start, operand_channel_width * operand_channel_width
        )
        linear = jnp.dot(products, decoder, preferred_element_type=jnp.float32) + pair_output_bias
        upstream = lax.dynamic_slice_in_dim(pair_output_gradient, first_row, rows_by_length, 0)
        upstream = upstream.reshape(rows_by_length * local_residue_start, channels).astype(
            jnp.float32
        )
        accumulate_slope_rows = (upstream * 2.0 * jnp.maximum(linear, 0.0)).astype(jnp.bfloat16)
        stored = lax.dynamic_update_slice_in_dim(
            stored,
            accumulate_slope_rows.reshape(rows_by_length, local_residue_start * channels),
            first_row,
            0,
        )
        accumulate_slopes = outer_slopes(accumulate_slope_rows, rows_by_length, local_residue_start)
        second_operand_gradient = second_operand_gradient + jnp.einsum(
            "ijcd,sic->sjd", accumulate_slopes, left_block, preferred_element_type=jnp.float32
        )
    second_operand_gradient, stored, right_whole = (second_operand_gradient, stored, right_whole)
    received = lax.all_to_all(stored, "col", split_axis=0, concat_axis=1, tiled=True)
    right_all = right_whole.reshape(alignment_row_count, residue_total_count, operand_channel_width)
    col_span = local_residue_start * max(
        max(1, 96 // local_residue_start), lax.axis_size("col") // 8
    )
    first_operand_gradient = jnp.zeros(
        (alignment_row_count, local_residue_start, operand_channel_width), jnp.float32
    )
    for offset in range(0, residue_total_count, col_span):
        width_cols = min(col_span, residue_total_count - offset)
        slope_rows = received[:, offset * channels : (offset + width_cols) * channels].reshape(
            local_residue_start * width_cols, channels
        )
        slopes = outer_slopes(slope_rows, local_residue_start, width_cols)
        first_operand_gradient = first_operand_gradient + jnp.einsum(
            "ijcd,sjd->sic",
            slopes,
            right_all[:, offset : offset + width_cols],
            preferred_element_type=jnp.float32,
        )
    first_operand_gradient_step = first_operand_gradient.astype(jnp.bfloat16).reshape(
        alignment_row_count * local_residue_start, operand_channel_width
    )
    second_operand_gradient_step = second_operand_gradient.astype(jnp.bfloat16).reshape(
        alignment_row_count * local_residue_start, operand_channel_width
    )
    alignment_gradient = jnp.dot(
        first_operand_gradient_step, left_factor_matrix.T, preferred_element_type=jnp.float32
    ) + jnp.dot(
        second_operand_gradient_step, right_factor_matrix.T, preferred_element_type=jnp.float32
    )
    alignment_gradient = alignment_gradient.astype(jnp.bfloat16).reshape(
        alignment_row_count, local_residue_start, alignment_channel_width
    )
    return (first_operand_gradient, second_operand_gradient, alignment_gradient)


def solution(mesh):
    placed = (P("group", "col", None), P(), P(), P(), P(), P("group", "col", None))
    return jax.shard_map(
        per_device,
        mesh=mesh,
        in_specs=placed,
        out_specs=(P("group", "col", None), P("group", "col", None), P("group", "col", None)),
        check_vma=False,
    )
```

profile of v0, /device:TPU:38, one launch (start us, length us, event | category | flops | bytes accessed | tf_op | source)
XLA Modules:
  0.0 278.4 jit_solution(2728740958674817468)
XLA Ops:
  7.3 1.0 reshape.97
  8.2 0.9 convolution_convert_fusion
  9.4 0.9 convolution_convert_fusion.1
  10.6 0.6 pad_maximum_fusion
  11.3 1.6 convert_multiply_fusion.2
  12.9 1.8 convert_multiply_fusion
  14.7 143.4 %all-gather.2.cloned.1.call-done = bf16[192,8192]{1,0:T(8,128)(2,1)} async-done(((bf16[192,128]{1,0:T(8,128)(2,1)}), bf16[192,8192]{1,0:T(8,128)(2,1)}) %all-gather.2.cloned.1.call-update) | async-done | bytes 3145744 | tf_op jit(solution)/shard_map/all_gather | solution.py:10
  158.1 2.1 fusion.42
  160.2 0.4 copy.28
  160.6 0.9 copy.30
  161.5 0.9 copy-done.3
  162.4 1.4 fusion.5
  163.8 5.4 %copy.31 = bf16[96,4,32,32]{3,2,1,0:T(8,128)(2,1)S(1)} copy(bf16[96,4,32,32]{0,3,2,1:T(8,128)(2,1)} %fusion.5) | data formatting | bytes 1572864 | tf_op jit(solution)/shard_map/convert_element_type | solution.py:84
  169.2 4.0 %reshape.105 = bf16[384,1024]{1,0:T(8,128)(2,1)} reshape(bf16[96,4,32,32]{3,2,1,0:T(8,128)(2,1)S(1)} %copy.31) | data formatting | bytes 1572864 | tf_op jit(solution)/shard_map/reshape | solution.py:84
  173.3 1.5 fusion.14
  174.8 0.7 reshape.106
  175.5 1.4 copy.24
  177.0 0.9 copy.26
  177.9 0.9 copy-done.5
  178.8 1.4 fusion.4
  180.2 5.4 %copy.27 = bf16[96,4,32,32]{3,2,1,0:T(8,128)(2,1)S(1)} copy(bf16[96,4,32,32]{0,3,2,1:T(8,128)(2,1)} %fusion.4) | data formatting | bytes 1572864 | tf_op jit(solution)/shard_map/convert_element_type | solution.py:84
  185.6 4.0 %reshape.102 = bf16[384,1024]{1,0:T(8,128)(2,1)} reshape(bf16[96,4,32,32]{3,2,1,0:T(8,128)(2,1)S(1)} %copy.27) | data formatting | bytes 1572864 | tf_op jit(solution)/shard_map/reshape | solution.py:84
  189.6 1.5 fusion.15
  191.1 0.7 reshape.103
  191.9 1.0 slice.45
  192.9 0.3 copy.32
  193.2 0.8 copy-done.6
  194.0 0.7 fusion.6
  194.6 3.2 %copy.35 = bf16[64,4,32,32]{3,2,1,0:T(8,128)(2,1)S(1)} copy(bf16[64,4,32,32]{0,3,2,1:T(8,128)(2,1)S(1)} %fusion.6) | data formatting | bytes 1048576 | tf_op jit(solution)/shard_map/convert_element_type | solution.py:84
  197.9 2.2 reshape.108
  200.2 0.3 fusion.18
  200.6 0.8 all_to_all.14
  201.4 14.5 %all-to-all-start = ((bf16[64,4,512]{2,1,0:T(4,128)(2,1)}), bf16[64,4,512]{2,1,0:T(4,128)(2,1)}, u32[]{:S(2)}, u32[]{:S(2)}) async-start(bf16[64,4,512]{2,1,0:T(4,128)(2,1)} %all_to_all.14), calls=%async_computation | async-start | bytes 524288 | tf_op jit(solution)/shard_map/all_to_all | solution.py:104
  216.0 2.7 split.5
  218.6 3.1 %copy.21 = bf16[96,8192]{0,1:T(8,128)(2,1)S(1)} copy(bf16[96,8192]{1,0:T(8,128)(2,1)} %split.5) | data formatting | bytes 3145728 | tf_op jit(solution)/shard_map/split | solution.py:11
  221.8 0.9 slice.49
  222.7 1.2 fusion.43
  223.8 2.8 %copy.72 = bf16[96,96,32]{1,0,2:T(8,128)(2,1)} copy(bf16[96,96,32]{0,2,1:T(8,128)(2,1)} %get-tuple-element.6) | data formatting | bytes 1179648
  226.6 1.8 copy.71
  228.4 1.3 multiply_convert_fusion.4
  229.7 3.8 %reshape.116 = bf16[96,4,32,32]{3,2,1,0:T(8,128)(2,1)S(1)} reshape(bf16[384,1024]{1,0:T(8,128)(2,1)} %multiply_convert_fusion.4) | data formatting | bytes 1572864 | tf_op jit(solution)/shard_map/reshape | solution.py:49
  233.5 1.3 multiply_convert_fusion.3
  234.7 4.9 %reshape.117 = bf16[96,4,32,32]{3,2,1,0:T(8,128)(2,1)} reshape(bf16[384,1024]{1,0:T(8,128)(2,1)} %multiply_convert_fusion.3) | data formatting | bytes 1572864 | tf_op jit(solution)/shard_map/reshape | solution.py:49
  239.7 1.1 fusion.8
  240.7 3.7 %reshape.118 = bf16[64,4,32,32]{3,2,1,0:T(8,128)(2,1)} reshape(bf16[256,1024]{1,0:T(8,128)(2,1)} %fusion.8) | data formatting | bytes 1048576 | tf_op jit(solution)/shard_map/reshape | solution.py:49
  244.5 4.7 %fusion.20 = f32[96,4,32]{0,2,1:T(8,128)S(1)} fusion(bf16[96,4,32,32]{3,2,1,0:T(8,128)(2,1)S(1)} %reshape.116, bf16[96,96,32]{1,0,2:T(8,128)(2,1)} %copy-done.5), kind=kOutput, calls=%fused_computation.34 | convolution fusion | flops 75497472 | bytes 1425408 | tf_op jit(solution)/shard_map/ijcd,sic->sjd/dot_general | solution.py:100
  249.2 3.5 %fusion.27 = f32[96,4,32]{0,2,1:T(8,128)S(1)} fusion(f32[96,4,32]{0,2,1:T(8,128)S(1)} %fusion.20, bf16[96,4,32,32]{3,2,1,0:T(8,128)(2,1)S(1)} %copy-done.1, bf16[96,96,32]{1,0,2:T(8,128)(2,1)S(1)} %copy-done.4), kind=kOutput, calls=%fused_computation.40 | convolution fusion | flops 75509760 | bytes 1474560 | tf_op jit(solution)/shard_map/ijcd,sic->sjd/dot_general | solution.py:100
  252.8 1.4 fusion.46
  254.2 3.3 %all-to-all-done = bf16[64,4,512]{2,1,0:T(4,128)(2,1)} async-done(((bf16[64,4,512]{2,1,0:T(4,128)(2,1)}), bf16[64,4,512]{2,1,0:T(4,128)(2,1)}, u32[]{:S(2)}, u32[]{:S(2)}) %all-to-all-start) | async-done | bytes 262176 | tf_op jit(solution)/shard_map/all_to_all | solution.py:104
  257.6 1.0 fusion.44
  258.6 0.9 slice.50
  259.6 0.4 multiply_convert_fusion.5
  259.9 0.4 copy.39
  260.3 0.6 reshape.113
  261.0 0.4 multiply_convert_fusion.6
  261.4 0.4 copy.36
  261.8 1.6 reshape.111
  263.5 0.3 fusion.7
  263.8 0.2 copy.42
  264.0 1.4 reshape.115
  265.4 2.1 convolution_bitcast_fusion.1
  267.5 0.8 fusion.30
  268.4 2.0 fusion.45
  270.8 0.7 reshape.121
  (59 shorter events, 1.8 us)
Async XLA Ops:
  7.2 166.1 %copy-start = (bf16[1024,128]{1,0:T(8,128)(2,1)S(1)}, bf16[1024,128]{1,0:T(8,128)(2,1)}, u32[]{:S(2)}) copy-start(bf16[1024,128]{1,0:T(8,128)(2,1)} %param.9) | copy-start | bytes 786436
  7.2 150.9 %all-gather.2.cloned.1.call-start = ((), (), s32[]{:S(2)}) async-start(), calls=%async_computation.1 | async-start | bytes 3194880 | tf_op jit(solution)/shard_map/all_gather | solution.py:10
  161.5 0.9 copy-start.3
  169.2 4.0 %copy-start.21 = (f32[128]{0:T(128)S(1)}, f32[128]{0:T(128)}, u32[]{:S(2)}) copy-start(f32[128]{0:T(128)} %param.10) | copy-start | bytes 1540
  177.9 0.9 copy-start.5
  191.1 0.7 copy-start.10
  193.2 0.8 copy-start.6
  197.9 2.3 copy-start.15
  197.9 2.6 copy-start.18
  197.9 2.7 copy-start.17
  200.5 18.2 %copy-start.13 = (bf16[256,128]{1,0:T(8,128)(2,1)}, bf16[256,128]{1,0:T(8,128)(2,1)S(1)}, u32[]{:S(2)}) copy-start(bf16[256,128]{1,0:T(8,128)(2,1)S(1)} %fusion.18) | copy-start | bytes 196612
  201.4 56.2 %all-to-all-start = ((bf16[64,4,512]{2,1,0:T(4,128)(2,1)}), bf16[64,4,512]{2,1,0:T(4,128)(2,1)}, u32[]{:S(2)}, u32[]{:S(2)}) async-start(bf16[64,4,512]{2,1,0:T(4,128)(2,1)} %all_to_all.14), calls=%async_computation | async-start | bytes 524288 | tf_op jit(solution)/shard_map/all_to_all | solution.py:104
  223.8 4.6 %copy-start.11 = (bf16[384,128]{1,0:T(8,128)(2,1)S(1)}, bf16[384,128]{1,0:T(8,128)(2,1)}, u32[]{:S(2)}) copy-start(bf16[384,128]{1,0:T(8,128)(2,1)} %copy-done.10) | copy-start | bytes 294916
  234.7 4.9 %copy-start.14 = (bf16[256,128]{1,0:T(8,128)(2,1)S(1)}, bf16[256,128]{1,0:T(8,128)(2,1)}, u32[]{:S(2)}) copy-start(bf16[256,128]{1,0:T(8,128)(2,1)} %copy-done.13) | copy-start | bytes 196612
  244.5 4.7 %copy-start.1 = (bf16[96,4,32,32]{3,2,1,0:T(8,128)(2,1)S(1)}, bf16[96,4,32,32]{3,2,1,0:T(8,128)(2,1)}, u32[]{:S(2)}) copy-start(bf16[96,4,32,32]{3,2,1,0:T(8,128)(2,1)} %reshape.117) | copy-start | bytes 2359300
  244.5 4.7 %copy-start.4 = (bf16[96,96,32]{1,0,2:T(8,128)(2,1)S(1)}, bf16[96,96,32]{1,0,2:T(8,128)(2,1)}, u32[]{:S(2)}) copy-start(bf16[96,96,32]{1,0,2:T(8,128)(2,1)} %copy-done.3) | copy-start | bytes 1769476
  249.2 3.6 %copy-start.2 = (bf16[64,4,32,32]{3,2,1,0:T(8,128)(2,1)S(1)}, bf16[64,4,32,32]{3,2,1,0:T(8,128)(2,1)}, u32[]{:S(2)}) copy-start(bf16[64,4,32,32]{3,2,1,0:T(8,128)(2,1)} %reshape.118) | copy-start | bytes 1572868
  249.2 3.6 %copy-start.7 = (bf16[96,2048]{0,1:T(8,128)(2,1)S(1)}, bf16[96,2048]{0,1:T(8,128)(2,1)}, u32[]{:S(2)}) copy-start(bf16[96,2048]{0,1:T(8,128)(2,1)} %copy-done.6) | copy-start | bytes 1179652
  264.0 3.5 %copy-start.8 = (bf16[4,96,32,32]{1,0,3,2:T(4,128)(2,1)S(1)}, bf16[4,96,32,32]{1,0,3,2:T(4,128)(2,1)}, u32[]{:S(2)}) copy-start(bf16[4,96,32,32]{1,0,3,2:T(4,128)(2,1)} %reshape.111) | copy-start | bytes 2359300
  265.4 2.1 copy-start.12
  265.4 2.9 %copy-start.9 = (bf16[4,64,32,32]{1,0,3,2:T(4,128)(2,1)S(1)}, bf16[4,64,32,32]{1,0,3,2:T(4,128)(2,1)}, u32[]{:S(2)}) copy-start(bf16[4,64,32,32]{1,0,3,2:T(4,128)(2,1)} %reshape.115) | copy-start | bytes 1572868
  265.4 2.9 %copy-start.16 = (bf16[96,64,32]{0,2,1:T(8,128)(2,1)S(1)}, bf16[96,64,32]{0,2,1:T(8,128)(2,1)}, u32[]{:S(2)}) copy-start(bf16[96,64,32]{0,2,1:T(8,128)(2,1)} %slice.49) | copy-start | bytes 1179652
  268.3 2.1 copy-start.19
  268.3 2.3 copy-start.20
Sparse Core Ops, SparseCore 0:
  11.4 146.6 all-gather.1
where the time goes:
time: 279 us; the launch traced here: 278 us
  waiting for transfers between devices  147 us (53%)
  local copies, waits for them, and re-layouts  70.5 us (25%)
  matrix products  28 us (10%)
  starting transfers between devices  14.6 us (5%)
  between operations  14.6 us (5%)
  other arithmetic  3.96 us (1%)
    all_gather x1, waiting for transfers between devices, in_one_piece(): whole = lax.all_gather(both, axis, axis=dim, tiled=True)  143 us
    reshape x6, local copies, waits for them, and re-layouts, outer_slopes(): backward.astype(jnp.bfloat16)  16 us
    all_to_all x1, starting transfers between devices, per_device(): lax.all_to_all(stored, 'col', split_axis=0, concat_axis=1, tiled=True)  14.5 us
    convert_element_type x3, local copies, waits for them, and re-layouts, per_device(): products.astype(jnp.bfloat16)  14 us
    reshape x3, local copies, waits for them, and re-layouts, per_device(): products.astype(jnp.bfloat16)  10.3 us
    dot_general x3, matrix products, per_device(): jnp.einsum('ijcd,sic->sjd', accumulate_slopes, left_block, preferred_elem...  9.6 us
    unnamed x46, local copies, waits for them, and re-layouts  7.3 us
    split x2, local copies, waits for them, and re-layouts, in_one_piece(): jnp.split(whole, [sum(widths[:k]) for k in range(1, len(widths))], axis=a...  5.78 us
  transfers between devices with their start and end apart: 2, of which 2 were waited for; matrix products, arithmetic and copies ran while one was open for 15% of the time, Pallas kernels for 0%

commit v1 on v0

--- a/solution.py
+++ b/solution.py
@@ -101,7 +101,10 @@
             "ijcd,sic->sjd", accumulate_slopes, left_block, preferred_element_type=jnp.float32
         )
     second_operand_gradient, stored, right_whole = (second_operand_gradient, stored, right_whole)
-    received = lax.all_to_all(stored, "col", split_axis=0, concat_axis=1, tiled=True)
+    received = jnp.concatenate(
+        lax.all_to_all(jnp.stack(jnp.split(stored, lax.axis_size("col"), axis=0)), "col", 0, 0),
+        axis=1,
+    )
     right_all = right_whole.reshape(alignment_row_count, residue_total_count, operand_channel_width)
     col_span = local_residue_start * max(
         max(1, 96 // local_residue_start), lax.axis_size("col") // 8

time: 279 us -> 364 us (1.30)
  local copies, waits for them, and re-layouts: 70.5 us -> 151 us
    unnamed x46 -> x183, local copies, waits for them, and re-layouts: 7.3 us -> 48.3 us
    another operation x0 -> x65, local copies, waits for them, and re-layouts: none -> 40.1 us  [per_device(): jnp.stack(jnp.split(stored, lax.axis_size('col'), axis=0))]
  transfers between devices with their start and end apart: 2 -> 2, of which waited for: 2 -> 2; matrix products, arithmetic and copies ran while one was open for 15% -> 12% of each run, Pallas kernels for 0% -> 0%
where the time goes in v1:
time: 364 us; the launch traced here: 360 us
  local copies, waits for them, and re-layouts  151 us (41%)
  waiting for transfers between devices  147 us (40%)
  matrix products  28.8 us (8%)
  between operations  15.2 us (4%)
  starting transfers between devices  14.4 us (4%)
  other arithmetic  3.94 us (1%)
    all_gather x1, waiting for transfers between devices, in_one_piece(): whole = lax.all_gather(both, axis, axis=dim, tiled=True)  143 us
    unnamed x183, local copies, waits for them, and re-layouts  48.3 us
    another operation x65, local copies, waits for them, and re-layouts, per_device(): jnp.stack(jnp.split(stored, lax.axis_size('col'), axis=0))  40.1 us
    reshape x6, local copies, waits for them, and re-layouts, outer_slopes(): backward.astype(jnp.bfloat16)  16.2 us
    convert_element_type x3, local copies, waits for them, and re-layouts, per_device(): products.astype(jnp.bfloat16)  14.5 us
    all_to_all x1, starting transfers between devices, per_device(): lax.all_to_all(jnp.stack(jnp.split(stored, lax.axis_size('col'), axis=0))...  14.3 us
    reshape x3, local copies, waits for them, and re-layouts, per_device(): products.astype(jnp.bfloat16)  10.3 us
    dot_general x3, matrix products, per_device(): jnp.einsum('ijcd,sic->sjd', accumulate_slopes, left_block, preferred_elem...  9.6 us
  transfers between devices with their start and end apart: 2, of which 2 were waited for; matrix products, arithmetic and copies ran while one was open for 12% of the time, Pallas kernels for 0%

profile of v1, /device:TPU:38, one launch (start us, length us, event | category | flops | bytes accessed | tf_op | source)
XLA Modules:
  0.0 360.2 jit_solution(6365624477995590271)
XLA Ops:
  7.3 1.0 reshape.222
  11.3 1.5 convert_multiply_fusion.2
  12.9 1.8 convert_multiply_fusion
  14.7 143.4 %all-gather.2.cloned.1.call-done = bf16[192,8192]{1,0:T(8,128)(2,1)} async-done(((bf16[192,128]{1,0:T(8,128)(2,1)}), bf16[192,8192]{1,0:T(8,128)(2,1)}) %all-gather.2.cloned.1.call-update) | async-done | bytes 3145744 | tf_op jit(solution)/shard_map/all_gather | solution.py:10
  158.1 2.2 fusion.42
  160.6 0.9 copy.26
  161.5 0.9 copy-done.3
  162.5 1.4 fusion.4
  163.8 5.8 %copy.27 = bf16[96,4,32,32]{3,2,1,0:T(8,128)(2,1)S(1)} copy(bf16[96,4,32,32]{0,3,2,1:T(8,128)(2,1)} %fusion.4) | data formatting | bytes 1572864 | tf_op jit(solution)/shard_map/convert_element_type | solution.py:84
  169.7 4.1 %reshape.227 = bf16[384,1024]{1,0:T(8,128)(2,1)} reshape(bf16[96,4,32,32]{3,2,1,0:T(8,128)(2,1)S(1)} %copy.27) | data formatting | bytes 1572864 | tf_op jit(solution)/shard_map/reshape | solution.py:84
  173.7 1.5 fusion.15
  176.6 1.4 copy.28
  179.8 1.4 fusion.5
  181.2 5.4 %copy.31 = bf16[96,4,32,32]{3,2,1,0:T(8,128)(2,1)S(1)} copy(bf16[96,4,32,32]{0,3,2,1:T(8,128)(2,1)} %fusion.5) | data formatting | bytes 1572864 | tf_op jit(solution)/shard_map/convert_element_type | solution.py:84
  186.6 4.0 %reshape.229 = bf16[384,1024]{1,0:T(8,128)(2,1)} reshape(bf16[96,4,32,32]{3,2,1,0:T(8,128)(2,1)S(1)} %copy.31) | data formatting | bytes 1572864 | tf_op jit(solution)/shard_map/reshape | solution.py:84
  190.6 1.6 fusion.14
  194.2 1.3 stack.196
  195.5 1.3 stack.197
  196.7 1.3 stack.198
  198.0 1.3 stack.199
  199.3 1.3 stack.200
  200.6 1.3 stack.201
  201.8 1.3 stack.202
  203.1 1.3 stack.203
  204.4 1.3 stack.204
  205.7 1.3 stack.205
  207.0 1.3 stack.206
  208.2 1.3 stack.207
  209.5 1.3 stack.208
  210.8 1.3 stack.209
  212.1 1.3 stack.210
  213.3 1.3 stack.211
  214.6 1.3 stack.212
  215.9 1.3 stack.213
  217.2 1.3 stack.214
  232.8 1.0 slice.173
  235.6 3.2 copy.35
  239.2 2.2 reshape.231
  241.5 0.9 fusion.18
  242.7 1.3 constant_dynamic-update-slice_fusion.62
  243.9 1.3 constant_dynamic-update-slice_fusion.61
  245.2 1.3 constant_dynamic-update-slice_fusion.60
  246.5 1.3 constant_dynamic-update-slice_fusion.59
  282.9 14.3 %all-to-all-start = ((bf16[64,4,512]{2,1,0:T(4,128)(2,1)}), bf16[64,4,512]{2,1,0:T(4,128)(2,1)}, u32[]{:S(2)}, u32[]{:S(2)}) async-start(bf16[64,4,512]{2,1,0:T(4,128)(2,1)} %constant_dynamic-update-slice_fusion), calls=%async_computation | async-start | bytes 524288 | tf_op jit(solution)/shard_map/all_to_all | solution.py:105
  297.3 2.7 split.261
  300.0 3.1 copy.21
  303.9 1.2 fusion.43
  305.1 2.9 copy.72
  308.0 1.8 copy.71
  309.8 1.3 multiply_convert_fusion.4
  311.2 3.8 %reshape.240 = bf16[96,4,32,32]{3,2,1,0:T(8,128)(2,1)S(1)} reshape(bf16[384,1024]{1,0:T(8,128)(2,1)} %multiply_convert_fusion.4) | data formatting | bytes 1572864 | tf_op jit(solution)/shard_map/reshape | solution.py:49
  315.0 1.3 multiply_convert_fusion.3
  316.2 4.9 %reshape.241 = bf16[96,4,32,32]{3,2,1,0:T(8,128)(2,1)} reshape(bf16[384,1024]{1,0:T(8,128)(2,1)} %multiply_convert_fusion.3) | data formatting | bytes 1572864 | tf_op jit(solution)/shard_map/reshape | solution.py:49
  321.1 1.1 fusion.8
  322.2 3.9 %reshape.242 = bf16[64,4,32,32]{3,2,1,0:T(8,128)(2,1)} reshape(bf16[256,1024]{1,0:T(8,128)(2,1)} %fusion.8) | data formatting | bytes 1048576 | tf_op jit(solution)/shard_map/reshape | solution.py:49
  326.2 4.7 %fusion.20 = f32[96,4,32]{0,2,1:T(8,128)S(1)} fusion(bf16[96,4,32,32]{3,2,1,0:T(8,128)(2,1)S(1)} %reshape.240, bf16[96,96,32]{1,0,2:T(8,128)(2,1)} %copy-done.3), kind=kOutput, calls=%fused_computation.34 | convolution fusion | flops 75497472 | bytes 1425408 | tf_op jit(solution)/shard_map/ijcd,sic->sjd/dot_general | solution.py:100
  330.9 3.5 fusion.27
  334.5 1.4 fusion.51
  335.9 3.2 all-to-all-done
  339.1 1.0 fusion.44
  343.3 1.6 reshape.235
  345.5 1.4 reshape.239
  347.0 2.1 convolution_bitcast_fusion.1
  349.9 2.0 fusion.50
  (259 shorter events, 66.7 us)
Async XLA Ops:
  7.2 166.6 %copy-start = (bf16[1024,128]{1,0:T(8,128)(2,1)S(1)}, bf16[1024,128]{1,0:T(8,128)(2,1)}, u32[]{:S(2)}) copy-start(bf16[1024,128]{1,0:T(8,128)(2,1)} %param.9) | copy-start | bytes 786436
  7.2 150.9 %all-gather.2.cloned.1.call-start = ((), (), s32[]{:S(2)}) async-start(), calls=%async_computation.1 | async-start | bytes 3194880 | tf_op jit(solution)/shard_map/all_gather | solution.py:10
  161.5 0.9 copy-start.3
  169.7 4.1 %copy-start.58 = (f32[128]{0:T(128)S(1)}, f32[128]{0:T(128)}, u32[]{:S(2)}) copy-start(f32[128]{0:T(128)} %param.10) | copy-start | bytes 1540
  178.9 0.9 copy-start.4
  192.3 0.6 copy-start.10
  234.1 0.8 copy-start.6
  238.8 2.6 copy-start.15
  238.9 8.9 %copy-start.57 = (bf16[1,4,512]{2,1,0:T(4,128)(2,1)S(1)}, bf16[1,4,512]{2,1,0:T(4,128)(2,1)}, u32[]{:S(2)}) copy-start(bf16[1,4,512]{2,1,0:T(4,128)(2,1)} %stack.200) | copy-start | bytes 12292
  238.9 9.5 %copy-start.56 = (bf16[1,4,512]{2,1,0:T(4,128)(2,1)S(1)}, bf16[1,4,512]{2,1,0:T(4,128)(2,1)}, u32[]{:S(2)}) copy-start(bf16[1,4,512]{2,1,0:T(4,128)(2,1)} %stack.201) | copy-start | bytes 12292
  238.9 10.1 %copy-start.55 = (bf16[1,4,512]{2,1,0:T(4,128)(2,1)S(1)}, bf16[1,4,512]{2,1,0:T(4,128)(2,1)}, u32[]{:S(2)}) copy-start(bf16[1,4,512]{2,1,0:T(4,128)(2,1)} %stack.202) | copy-start | bytes 12292
  238.9 10.7 %copy-start.54 = (bf16[1,4,512]{2,1,0:T(4,128)(2,1)S(1)}, bf16[1,4,512]{2,1,0:T(4,128)(2,1)}, u32[]{:S(2)}) copy-start(bf16[1,4,512]{2,1,0:T(4,128)(2,1)} %stack.203) | copy-start | bytes 12292
  238.9 11.3 %copy-start.53 = (bf16[1,4,512]{2,1,0:T(4,128)(2,1)S(1)}, bf16[1,4,512]{2,1,0:T(4,128)(2,1)}, u32[]{:S(2)}) copy-start(bf16[1,4,512]{2,1,0:T(4,128)(2,1)} %stack.204) | copy-start | bytes 12292
  238.9 11.9 %copy-start.52 = (bf16[1,4,512]{2,1,0:T(4,128)(2,1)S(1)}, bf16[1,4,512]{2,1,0:T(4,128)(2,1)}, u32[]{:S(2)}) copy-start(bf16[1,4,512]{2,1,0:T(4,128)(2,1)} %stack.205) | copy-start | bytes 12292
  238.9 12.4 %copy-start.51 = (bf16[1,4,512]{2,1,0:T(4,128)(2,1)S(1)}, bf16[1,4,512]{2,1,0:T(4,128)(2,1)}, u32[]{:S(2)}) copy-start(bf16[1,4,512]{2,1,0:T(4,128)(2,1)} %stack.206) | copy-start | bytes 12292
  238.9 13.0 %copy-start.50 = (bf16[1,4,512]{2,1,0:T(4,128)(2,1)S(1)}, bf16[1,4,512]{2,1,0:T(4,128)(2,1)}, u32[]{:S(2)}) copy-start(bf16[1,4,512]{2,1,0:T(4,128)(2,1)} %stack.207) | copy-start | bytes 12292
  238.9 13.6 %copy-start.49 = (bf16[1,4,512]{2,1,0:T(4,128)(2,1)S(1)}, bf16[1,4,512]{2,1,0:T(4,128)(2,1)}, u32[]{:S(2)}) copy-start(bf16[1,4,512]{2,1,0:T(4,128)(2,1)} %stack.208) | copy-start | bytes 12292
  238.9 14.2 %copy-start.48 = (bf16[1,4,512]{2,1,0:T(4,128)(2,1)S(1)}, bf16[1,4,512]{2,1,0:T(4,128)(2,1)}, u32[]{:S(2)}) copy-start(bf16[1,4,512]{2,1,0:T(4,128)(2,1)} %stack.209) | copy-start | bytes 12292
  239.0 14.8 %copy-start.47 = (bf16[1,4,512]{2,1,0:T(4,128)(2,1)S(1)}, bf16[1,4,512]{2,1,0:T(4,128)(2,1)}, u32[]{:S(2)}) copy-start(bf16[1,4,512]{2,1,0:T(4,128)(2,1)} %stack.210) | copy-start | bytes 12292
  239.0 15.4 %copy-start.46 = (bf16[1,4,512]{2,1,0:T(4,128)(2,1)S(1)}, bf16[1,4,512]{2,1,0:T(4,128)(2,1)}, u32[]{:S(2)}) copy-start(bf16[1,4,512]{2,1,0:T(4,128)(2,1)} %stack.211) | copy-start | bytes 12292
  239.0 15.9 %copy-start.45 = (bf16[1,4,512]{2,1,0:T(4,128)(2,1)S(1)}, bf16[1,4,512]{2,1,0:T(4,128)(2,1)}, u32[]{:S(2)}) copy-start(bf16[1,4,512]{2,1,0:T(4,128)(2,1)} %stack.212) | copy-start | bytes 12292
  239.0 16.5 %copy-start.44 = (bf16[1,4,512]{2,1,0:T(4,128)(2,1)S(1)}, bf16[1,4,512]{2,1,0:T(4,128)(2,1)}, u32[]{:S(2)}) copy-start(bf16[1,4,512]{2,1,0:T(4,128)(2,1)} %stack.213) | copy-start | bytes 12292
  239.0 17.1 %copy-start.43 = (bf16[1,4,512]{2,1,0:T(4,128)(2,1)S(1)}, bf16[1,4,512]{2,1,0:T(4,128)(2,1)}, u32[]{:S(2)}) copy-start(bf16[1,4,512]{2,1,0:T(4,128)(2,1)} %stack.214) | copy-start | bytes 12292
  239.0 17.7 %copy-start.42 = (bf16[1,4,512]{2,1,0:T(4,128)(2,1)S(1)}, bf16[1,4,512]{2,1,0:T(4,128)(2,1)}, u32[]{:S(2)}) copy-start(bf16[1,4,512]{2,1,0:T(4,128)(2,1)} %stack.215) | copy-start | bytes 12292
  239.0 18.3 %copy-start.41 = (bf16[1,4,512]{2,1,0:T(4,128)(2,1)S(1)}, bf16[1,4,512]{2,1,0:T(4,128)(2,1)}, u32[]{:S(2)}) copy-start(bf16[1,4,512]{2,1,0:T(4,128)(2,1)} %stack.216) | copy-start | bytes 12292
  239.0 18.9 %copy-start.39 = (bf16[1,4,512]{2,1,0:T(4,128)(2,1)S(1)}, bf16[1,4,512]{2,1,0:T(4,128)(2,1)}, u32[]{:S(2)}) copy-start(bf16[1,4,512]{2,1,0:T(4,128)(2,1)} %stack.217) | copy-start | bytes 12292
  239.0 19.5 %copy-start.40 = (bf16[1,4,512]{2,1,0:T(4,128)(2,1)S(1)}, bf16[1,4,512]{2,1,0:T(4,128)(2,1)}, u32[]{:S(2)}) copy-start(bf16[1,4,512]{2,1,0:T(4,128)(2,1)} %stack.218) | copy-start | bytes 12292
  239.0 20.1 %copy-start.38 = (bf16[1,4,512]{2,1,0:T(4,128)(2,1)S(1)}, bf16[1,4,512]{2,1,0:T(4,128)(2,1)}, u32[]{:S(2)}) copy-start(bf16[1,4,512]{2,1,0:T(4,128)(2,1)} %stack.219) | copy-start | bytes 12292
  239.1 20.7 %copy-start.37 = (bf16[1,4,512]{2,1,0:T(4,128)(2,1)S(1)}, bf16[1,4,512]{2,1,0:T(4,128)(2,1)}, u32[]{:S(2)}) copy-start(bf16[1,4,512]{2,1,0:T(4,128)(2,1)} %stack.220) | copy-start | bytes 12292
  239.1 21.2 %copy-start.36 = (bf16[1,4,512]{2,1,0:T(4,128)(2,1)S(1)}, bf16[1,4,512]{2,1,0:T(4,128)(2,1)}, u32[]{:S(2)}) copy-start(bf16[1,4,512]{2,1,0:T(4,128)(2,1)} %stack.221) | copy-start | bytes 12292
  239.1 21.8 %copy-start.34 = (bf16[1,4,512]{2,1,0:T(4,128)(2,1)S(1)}, bf16[1,4,512]{2,1,0:T(4,128)(2,1)}, u32[]{:S(2)}) copy-start(bf16[1,4,512]{2,1,0:T(4,128)(2,1)} %stack.222) | copy-start | bytes 12292
  239.1 22.4 %copy-start.35 = (bf16[1,4,512]{2,1,0:T(4,128)(2,1)S(1)}, bf16[1,4,512]{2,1,0:T(4,128)(2,1)}, u32[]{:S(2)}) copy-start(bf16[1,4,512]{2,1,0:T(4,128)(2,1)} %stack.223) | copy-start | bytes 12292
  239.1 23.0 %copy-start.33 = (bf16[1,4,512]{2,1,0:T(4,128)(2,1)S(1)}, bf16[1,4,512]{2,1,0:T(4,128)(2,1)}, u32[]{:S(2)}) copy-start(bf16[1,4,512]{2,1,0:T(4,128)(2,1)} %stack.224) | copy-start | bytes 12292
  239.1 23.6 %copy-start.32 = (bf16[1,4,512]{2,1,0:T(4,128)(2,1)S(1)}, bf16[1,4,512]{2,1,0:T(4,128)(2,1)}, u32[]{:S(2)}) copy-start(bf16[1,4,512]{2,1,0:T(4,128)(2,1)} %stack.225) | copy-start | bytes 12292
  239.1 24.2 %copy-start.31 = (bf16[1,4,512]{2,1,0:T(4,128)(2,1)S(1)}, bf16[1,4,512]{2,1,0:T(4,128)(2,1)}, u32[]{:S(2)}) copy-start(bf16[1,4,512]{2,1,0:T(4,128)(2,1)} %stack.226) | copy-start | bytes 12292
  239.1 24.8 %copy-start.30 = (bf16[1,4,512]{2,1,0:T(4,128)(2,1)S(1)}, bf16[1,4,512]{2,1,0:T(4,128)(2,1)}, u32[]{:S(2)}) copy-start(bf16[1,4,512]{2,1,0:T(4,128)(2,1)} %stack.227) | copy-start | bytes 12292
  239.1 25.3 %copy-start.29 = (bf16[1,4,512]{2,1,0:T(4,128)(2,1)S(1)}, bf16[1,4,512]{2,1,0:T(4,128)(2,1)}, u32[]{:S(2)}) copy-start(bf16[1,4,512]{2,1,0:T(4,128)(2,1)} %stack.228) | copy-start | bytes 12292
  239.1 25.9 %copy-start.28 = (bf16[1,4,512]{2,1,0:T(4,128)(2,1)S(1)}, bf16[1,4,512]{2,1,0:T(4,128)(2,1)}, u32[]{:S(2)}) copy-start(bf16[1,4,512]{2,1,0:T(4,128)(2,1)} %stack.229) | copy-start | bytes 12292
  239.2 26.5 %copy-start.27 = (bf16[1,4,512]{2,1,0:T(4,128)(2,1)S(1)}, bf16[1,4,512]{2,1,0:T(4,128)(2,1)}, u32[]{:S(2)}) copy-start(bf16[1,4,512]{2,1,0:T(4,128)(2,1)} %stack.230) | copy-start | bytes 12292
  239.2 27.1 %copy-start.26 = (bf16[1,4,512]{2,1,0:T(4,128)(2,1)S(1)}, bf16[1,4,512]{2,1,0:T(4,128)(2,1)}, u32[]{:S(2)}) copy-start(bf16[1,4,512]{2,1,0:T(4,128)(2,1)} %stack.231) | copy-start | bytes 12292
  239.2 27.7 %copy-start.25 = (bf16[1,4,512]{2,1,0:T(4,128)(2,1)S(1)}, bf16[1,4,512]{2,1,0:T(4,128)(2,1)}, u32[]{:S(2)}) copy-start(bf16[1,4,512]{2,1,0:T(4,128)(2,1)} %stack.232) | copy-start | bytes 12292
  239.2 28.3 %copy-start.24 = (bf16[1,4,512]{2,1,0:T(4,128)(2,1)S(1)}, bf16[1,4,512]{2,1,0:T(4,128)(2,1)}, u32[]{:S(2)}) copy-start(bf16[1,4,512]{2,1,0:T(4,128)(2,1)} %stack.233) | copy-start | bytes 12292
  239.2 28.9 %copy-start.23 = (bf16[1,4,512]{2,1,0:T(4,128)(2,1)S(1)}, bf16[1,4,512]{2,1,0:T(4,128)(2,1)}, u32[]{:S(2)}) copy-start(bf16[1,4,512]{2,1,0:T(4,128)(2,1)} %stack.234) | copy-start | bytes 12292
  239.2 29.5 %copy-start.22 = (bf16[1,4,512]{2,1,0:T(4,128)(2,1)S(1)}, bf16[1,4,512]{2,1,0:T(4,128)(2,1)}, u32[]{:S(2)}) copy-start(bf16[1,4,512]{2,1,0:T(4,128)(2,1)} %stack.235) | copy-start | bytes 12292
  239.2 30.0 %copy-start.21 = (bf16[1,4,512]{2,1,0:T(4,128)(2,1)S(1)}, bf16[1,4,512]{2,1,0:T(4,128)(2,1)}, u32[]{:S(2)}) copy-start(bf16[1,4,512]{2,1,0:T(4,128)(2,1)} %stack.236) | copy-start | bytes 12292
  239.2 30.6 %copy-start.20 = (bf16[1,4,512]{2,1,0:T(4,128)(2,1)S(1)}, bf16[1,4,512]{2,1,0:T(4,128)(2,1)}, u32[]{:S(2)}) copy-start(bf16[1,4,512]{2,1,0:T(4,128)(2,1)} %stack.237) | copy-start | bytes 12292
  239.2 31.2 %copy-start.19 = (bf16[1,4,512]{2,1,0:T(4,128)(2,1)S(1)}, bf16[1,4,512]{2,1,0:T(4,128)(2,1)}, u32[]{:S(2)}) copy-start(bf16[1,4,512]{2,1,0:T(4,128)(2,1)} %stack.238) | copy-start | bytes 12292
  242.4 57.5 %copy-start.13 = (bf16[256,128]{1,0:T(8,128)(2,1)}, bf16[256,128]{1,0:T(8,128)(2,1)S(1)}, u32[]{:S(2)}) copy-start(bf16[256,128]{1,0:T(8,128)(2,1)S(1)} %fusion.18) | copy-start | bytes 196612
  282.9 56.2 %all-to-all-start = ((bf16[64,4,512]{2,1,0:T(4,128)(2,1)}), bf16[64,4,512]{2,1,0:T(4,128)(2,1)}, u32[]{:S(2)}, u32[]{:S(2)}) async-start(bf16[64,4,512]{2,1,0:T(4,128)(2,1)} %constant_dynamic-update-slice_fusion), calls=%async_computation | async-start | bytes 524288 | tf_op jit(solution)/shard_map/all_to_all | solution.py:105
  311.2 3.8 %copy-start.11 = (bf16[384,128]{1,0:T(8,128)(2,1)S(1)}, bf16[384,128]{1,0:T(8,128)(2,1)}, u32[]{:S(2)}) copy-start(bf16[384,128]{1,0:T(8,128)(2,1)} %copy-done.10) | copy-start | bytes 294916
  316.2 4.9 %copy-start.14 = (bf16[256,128]{1,0:T(8,128)(2,1)S(1)}, bf16[256,128]{1,0:T(8,128)(2,1)}, u32[]{:S(2)}) copy-start(bf16[256,128]{1,0:T(8,128)(2,1)} %copy-done.13) | copy-start | bytes 196612
  326.1 4.7 %copy-start.1 = (bf16[96,4,32,32]{3,2,1,0:T(8,128)(2,1)S(1)}, bf16[96,4,32,32]{3,2,1,0:T(8,128)(2,1)}, u32[]{:S(2)}) copy-start(bf16[96,4,32,32]{3,2,1,0:T(8,128)(2,1)} %reshape.241) | copy-start | bytes 2359300
  326.1 4.7 %copy-start.5 = (bf16[96,96,32]{1,0,2:T(8,128)(2,1)S(1)}, bf16[96,96,32]{1,0,2:T(8,128)(2,1)}, u32[]{:S(2)}) copy-start(bf16[96,96,32]{1,0,2:T(8,128)(2,1)} %copy-done.4) | copy-start | bytes 1769476
  330.9 3.6 copy-start.2
  330.9 3.6 copy-start.7
  345.5 3.6 copy-start.8
  347.0 2.1 copy-start.12
  347.0 2.9 copy-start.9
  347.0 2.9 copy-start.16
  349.9 2.1 copy-start.17
  349.9 2.3 copy-start.18
Sparse Core Ops, SparseCore 0:
  11.4 146.6 all-gather.1
